TPU v7x, 256 devices: a whole 4x4x8 slice. The times are simulated.
256 devices in a mesh: dp: 8 (over z), mp: 32 (over y, x, core).
Axes of the slice: x: 4, y: 4, z: 8, core: 2. Of those that a mesh axis runs over, the one named last changes fastest.
Arguments:
- behaviors: bfloat16 [64, 2048, 1024], P('dp', 'mp'), may hold values from -8 to 8
- candidates: bfloat16 [64, 2048, 128], P('dp', 'mp'), may hold values from -12 to 12
- lengths: int32 [64], P('dp'), may hold values from 128 to 1024
- bilinear: bfloat16 [2048, 2048], P('mp'), may hold values from -1 to 2
- norm_gain: float32 [2048], replicated, may hold values from 0.1 to 1.9
- w_gate: bfloat16 [2048, 8192], P('dp', 'mp'), may hold values from -0.125 to 0.125
- w_up: bfloat16 [2048, 8192], P('dp', 'mp'), may hold values from -0.125 to 0.125
- w_down: bfloat16 [8192, 2048], P('mp', 'dp'), may hold values from -0.0625 to 0.0625
Outputs:
- interest: bfloat16 [64, 2048, 128], P('dp', 'mp')
All inputs are finite; a program needn't handle non-finite values.
Results may differ from a plain program's by a relative error of at most 0.015.
Values may be sent and summed in bfloat16 or wider, within the bound.
A program may use at most 64 MiB of HBM per device.

v0:
```python
import math

import jax
import jax.numpy as jnp
from jax import lax
from jax.sharding import Mesh
from jax.sharding import PartitionSpec as P

MP = ("mp_0", "mp_1", "mp_2")


def copy_for_each(value, axis):
    copies = jnp.broadcast_to(value, (lax.axis_size(axis), *value.shape))
    return lax.all_to_all(copies, axis, split_axis=0, concat_axis=0, tiled=True)


def joined_along(pieces, dim):
    dims = list(pieces.shape[1:])
    dims[dim] *= pieces.shape[0]
    return jnp.moveaxis(pieces, 0, dim).reshape(dims)


def gather_axes(value, axes, dim):
    far, near = axes
    initial = copy_for_each(value, far)
    pieces = jnp.swapaxes(copy_for_each(initial, near), 0, 1)
    return joined_along(pieces.reshape(-1, *value.shape), dim)


def cut_along(value, dim, peers):
    dims = value.shape
    pieces = value.reshape(*dims[:dim], peers, dims[dim] // peers, *dims[dim + 1 :])
    return jnp.moveaxis(pieces, dim, 0)


def sent_and_summed(value, axis, dim):
    pieces = cut_along(value, dim, lax.axis_size(axis))
    arrived = lax.all_to_all(pieces, axis, split_axis=0, concat_axis=0, tiled=True)
    return arrived.sum(axis=0)


def sum_in_two_steps(value, axes, dim):
    far, near = axes
    own = sent_and_summed(cut_along(value, dim, lax.axis_size(far)), near, dim + 1)
    return jnp.sum(lax.all_to_all(own, far, 0, 0, tiled=True), axis=0)


def side_by_side(arrays, axis, dim, along):
    both = jnp.concatenate(arrays, axis=along)
    result, at, gathered = (lax.all_gather(both, axis, axis=dim, tiled=True), 0, [])
    for a in arrays:
        gathered.append(lax.slice_in_dim(result, at, at + a.shape[along], axis=along))
        at += a.shape[along]
    return tuple(gathered)


def gathered_copies(value, axis, dim):
    return joined_along(copy_for_each(value, axis), dim)


def sent_and_summed_2(value, axis, dim):
    pieces = cut_along(value, dim, lax.axis_size(axis))
    arrived = lax.all_to_all(pieces, axis, split_axis=0, concat_axis=0, tiled=True)
    return arrived.astype(jnp.float32).sum(axis=0)


def sum_in_two_steps_2(value, axes, dim):
    far, near = axes
    own = sent_and_summed_2(cut_along(value, dim, lax.axis_size(far)), near, dim + 1)
    return jnp.sum(
        lax.all_to_all(own.astype(jnp.bfloat16), far, 0, 0, tiled=True).astype(jnp.float32), axis=0
    )


def attention_weights(scores, live):
    masked = jnp.where(live, scores, -1e30)
    highest = jnp.max(masked, axis=-1, keepdims=True)
    expons = jnp.where(live, jnp.exp(masked - highest), 0.0)
    return (expons / jnp.sum(expons, axis=-1, keepdims=True)).astype(jnp.bfloat16)


def shards(behaviors, candidates, lengths, bilinear, norm_gain, w_gate, w_up, w_down):
    user_count, width_part, cand_count = candidates.shape
    feature_width = bilinear.shape[1]
    behavior_count = behaviors.shape[2]
    query_part = jnp.einsum(
        "ek,ukc->uec",
        bilinear,
        gather_axes(candidates, (("mp_0", "mp_1"), "mp_2"), 1),
        preferred_element_type=jnp.float32,
    )
    query = query_part.astype(jnp.bfloat16)
    partial_value = jnp.einsum("ukc,ukl->ucl", query, behaviors, preferred_element_type=jnp.float32)
    scale = 1.0 / math.sqrt(feature_width)
    live = (
        lax.broadcasted_iota(jnp.int32, (user_count, 1, behavior_count), 2) < lengths[:, None, None]
    )
    share = sum_in_two_steps(partial_value, (("mp_0", "mp_1"), "mp_2"), 1)
    probs_share = attention_weights(share * scale, live)
    probs = gather_axes(probs_share, (("mp_0", "mp_1"), "mp_2"), 1)
    pooled = jnp.einsum(
        "ucl,ukl->ukc", probs, behaviors, preferred_element_type=jnp.float32
    ).astype(jnp.bfloat16)
    whole = gather_axes(pooled, (("mp_0", "mp_1"), "mp_2"), 1)
    values = whole.astype(jnp.float32)
    square_mean = jnp.mean(values * values, axis=1, keepdims=True)
    normed = (values * lax.rsqrt(square_mean + 1e-06) * norm_gain[None, :, None]).astype(
        jnp.bfloat16
    )
    pieces = side_by_side((w_gate, w_up), "dp", 0, 1)
    gate = jnp.einsum("ukc,kf->ucf", normed, pieces[0], preferred_element_type=jnp.float32)
    upward = jnp.einsum("ukc,kf->ucf", normed, pieces[1], preferred_element_type=jnp.float32)
    hidden = (jax.nn.silu(gate) * upward).astype(jnp.bfloat16)
    down_full = gathered_copies(w_down, "dp", 1)
    result = sum_in_two_steps_2(
        jnp.einsum("ucf,fk->kuc", hidden, down_full, preferred_element_type=jnp.float32).astype(
            jnp.bfloat16
        ),
        (("mp_0", "mp_1"), "mp_2"),
        0,
    )
    return jnp.transpose(result, (1, 0, 2)).astype(jnp.bfloat16)


def solution(mesh):
    finer = Mesh(mesh.devices.reshape(mesh.shape["dp"], 4, 4, 2), ("dp", "mp_0", "mp_1", "mp_2"))
    return jax.shard_map(
        shards,
        mesh=finer,
        in_specs=(
            P("dp", MP, None),
            P("dp", MP, None),
            P("dp"),
            P(MP, None),
            P(),
            P("dp", MP),
            P("dp", MP),
            P(MP, "dp"),
        ),
        out_specs=P("dp", MP, None),
        check_vma=False,
    )
```

profile of v0, /device:TPU:8, one launch (start us, length us, event | category | flops | bytes accessed | tf_op | source)
XLA Modules:
  0.0 315.4 jit_solution(13897474004266264887)
XLA Ops:
  6.5 0.0 copy-start
  6.5 1.5 broadcast_in_dim.45
  8.0 33.0 %all_to_all.55 = bf16[16,8,64,128]{3,2,1,0:T(8,128)(2,1)S(1)} all-to-all(bf16[16,8,64,128]{3,2,1,0:T(8,128)(2,1)S(1)} %broadcast_in_dim.45), channel_id=1, replica_groups=mesh['dp'=8,'mp_0'=4,'mp_1'=4,'mp_2'=2] {'mp_0','mp_1'}, dimensions={0} | all-to-all | bytes 4194304 | tf_op jit(solution)/shard_map/all_to_all | solution.py:14
  41.0 1.3 broadcast_in_dim.46
  42.4 7.1 %all_to_all.56 = bf16[2,16,8,64,128]{4,3,2,1,0:T(8,128)(2,1)S(1)} all-to-all(bf16[2,16,8,64,128]{4,3,2,1,0:T(8,128)(2,1)S(1)} %broadcast_in_dim.46), channel_id=1, replica_groups=mesh['dp'=8,'mp_0'=4,'mp_1'=4,'mp_2'=2] {'mp_2'}, dimensions={0} | all-to-all | bytes 8388608 | tf_op jit(solution)/shard_map/all_to_all | solution.py:14
  49.5 1.5 copy.55
  51.0 0.0 copy-start.3
  51.0 2.9 copy.56
  53.9 0.0 copy-done
  53.9 0.0 copy-done.3
  53.9 5.5 %convolution_bitcast_fusion = f32[8,16,8,1024]{3,2,1,0:T(8,128)} fusion(bf16[8,64,1024]{2,1,0:T(8,128)(2,1)S(1)} %copy-done, bf16[8,2048,128]{2,1,0:T(8,128)(2,1)} %bitcast.58, bf16[64,2048]{1,0:T(8,128)(2,1)S(1)} %copy-done.3), kind=kOutput, calls=%fused_computation.8 | convolution fusion | flops 402718720 | bytes 9699328 | tf_op jit(solution)/shard_map/ukc,ukl->ucl/dot_general | solution.py:93
  59.5 5.4 %copy.57 = f32[8,16,8,1024]{3,0,2,1:T(8,128)S(1)} copy(f32[8,16,8,1024]{3,2,1,0:T(8,128)} %convolution_bitcast_fusion) | data formatting | bytes 8388608 | tf_op jit(solution)/shard_map/reshape | solution.py:32
  64.9 2.7 copy.58
  67.6 8.2 %all_to_all.57 = f32[2,16,8,4,1024]{4,3,1,2,0:T(4,128)} all-to-all(f32[2,16,8,4,1024]{4,3,1,2,0:T(4,128)S(1)} %copy.58), channel_id=1, replica_groups=mesh['dp'=8,'mp_0'=4,'mp_1'=4,'mp_2'=2] {'mp_2'}, dimensions={0} | all-to-all | bytes 8388608 | tf_op jit(solution)/shard_map/all_to_all | solution.py:38
  75.8 4.2 %reduce_sum.60 = f32[16,8,4,1024]{3,2,0,1:T(4,128)S(1)} reduce(f32[2,16,8,4,1024]{4,3,1,2,0:T(4,128)} %all_to_all.57, f32[]{:T(128)} %constant.4.clone.1), dimensions={0}, to_apply=%region_0.0 | reduce | flops 524288 | bytes 6291460 | tf_op jit(solution)/shard_map/reduce_sum | solution.py:39
  80.0 0.0 copy-start.8
  80.0 1.6 copy.60
  81.6 6.2 %all-to-all-start.3 = ((f32[16,8,4,1024]{3,2,1,0:T(4,128)}), f32[16,8,4,1024]{3,2,1,0:T(4,128)S(1)}, u32[]{:S(2)}, u32[]{:S(2)}) async-start(f32[16,8,4,1024]{3,2,1,0:T(4,128)} %copy.60), calls=%async_computation.3 | async-start | bytes 4194304 | tf_op jit(solution)/shard_map/all_to_all | solution.py:45
  87.8 0.0 copy-done.8
  87.8 0.1 iota_compare_fusion
  87.9 32.2 %all-to-all-done.3 = f32[16,8,4,1024]{3,2,1,0:T(4,128)S(1)} async-done(((f32[16,8,4,1024]{3,2,1,0:T(4,128)}), f32[16,8,4,1024]{3,2,1,0:T(4,128)S(1)}, u32[]{:S(2)}, u32[]{:S(2)}) %all-to-all-start.3) | async-done | bytes 2097184 | tf_op jit(solution)/shard_map/all_to_all | solution.py:45
  120.2 0.5 reduce_sum.61
  120.7 0.2 fusion.32
  120.9 0.1 divide_convert_fusion
  121.0 0.4 broadcast_in_dim.49
  121.4 19.5 %all_to_all.58 = bf16[16,8,4,1024]{3,2,1,0:T(4,128)(2,1)S(1)} all-to-all(bf16[16,8,4,1024]{3,2,1,0:T(4,128)(2,1)S(1)} %broadcast_in_dim.49), channel_id=1, replica_groups=mesh['dp'=8,'mp_0'=4,'mp_1'=4,'mp_2'=2] {'mp_0','mp_1'}, dimensions={0} | all-to-all | bytes 2097152 | tf_op jit(solution)/shard_map/all_to_all | solution.py:14
  140.9 0.4 copy.61
  141.3 0.0 copy-start.4
  141.3 0.8 broadcast_in_dim.50
  142.1 5.4 %all_to_all.59 = bf16[2,16,8,4,1024]{4,3,1,2,0:T(4,128)(2,1)S(1)} all-to-all(bf16[2,16,8,4,1024]{4,3,1,2,0:T(4,128)(2,1)S(1)} %broadcast_in_dim.50), channel_id=1, replica_groups=mesh['dp'=8,'mp_0'=4,'mp_1'=4,'mp_2'=2] {'mp_2'}, dimensions={0} | all-to-all | bytes 4194304 | tf_op jit(solution)/shard_map/all_to_all | solution.py:14
  147.5 0.0 copy-done.4
  147.5 1.1 broadcast_in_dim.53
  148.6 8.5 %all-to-all-start.8 = ((bf16[8,256,256]{2,1,0:T(8,128)(2,1)}), bf16[8,256,256]{2,1,0:T(8,128)(2,1)}, u32[]{:S(2)}, u32[]{:S(2)}) async-start(bf16[8,256,256]{2,1,0:T(8,128)(2,1)} %broadcast_in_dim.53), calls=%async_computation.8 | async-start | bytes 2097152 | tf_op jit(solution)/shard_map/all_to_all | solution.py:14
  157.0 1.7 copy.62
  158.8 1.4 fusion.13
  160.2 0.0 copy-start.5
  160.2 0.0 copy-start.6
  160.2 26.0 %all-to-all-done.8 = bf16[8,256,256]{2,1,0:T(8,128)(2,1)} async-done(((bf16[8,256,256]{2,1,0:T(8,128)(2,1)}), bf16[8,256,256]{2,1,0:T(8,128)(2,1)}, u32[]{:S(2)}, u32[]{:S(2)}) %all-to-all-start.8) | async-done | bytes 1048608 | tf_op jit(solution)/shard_map/all_to_all | solution.py:14
  186.2 1.9 broadcast_in_dim.51
  188.1 6.1 %all-to-all-start.6 = ((bf16[16,8,64,128]{3,2,1,0:T(8,128)(2,1)}), bf16[16,8,64,128]{3,2,1,0:T(8,128)(2,1)S(1)}, u32[]{:S(2)}, u32[]{:S(2)}) async-start(bf16[16,8,64,128]{3,2,1,0:T(8,128)(2,1)} %broadcast_in_dim.51), calls=%async_computation.6 | async-start | bytes 4194304 | tf_op jit(solution)/shard_map/all_to_all | solution.py:14
  194.2 0.0 all-gather.2.cloned.1.call-start
  194.2 0.7 pad_maximum_fusion
  195.0 0.0 all-gather.2.cloned.1.call-update
  195.0 1.8 copy.68
  196.8 1.3 reshape.70
  198.1 27.8 %all-to-all-done.6 = bf16[16,8,64,128]{3,2,1,0:T(8,128)(2,1)S(1)} async-done(((bf16[16,8,64,128]{3,2,1,0:T(8,128)(2,1)}), bf16[16,8,64,128]{3,2,1,0:T(8,128)(2,1)S(1)}, u32[]{:S(2)}, u32[]{:S(2)}) %all-to-all-start.6) | async-done | bytes 2097184 | tf_op jit(solution)/shard_map/all_to_all | solution.py:14
  225.9 0.2 copy.64
  226.1 1.1 broadcast_in_dim.52
  227.2 7.1 %all_to_all.60 = bf16[2,16,8,64,128]{4,3,1,2,0:T(8,128)(2,1)S(1)} all-to-all(bf16[2,16,8,64,128]{4,3,1,2,0:T(8,128)(2,1)S(1)} %broadcast_in_dim.52), channel_id=1, replica_groups=mesh['dp'=8,'mp_0'=4,'mp_1'=4,'mp_2'=2] {'mp_2'}, dimensions={0} | all-to-all | bytes 8388608 | tf_op jit(solution)/shard_map/all_to_all | solution.py:14
  234.3 1.1 convert_bitcast_fusion
  235.4 1.7 copy.65
  237.0 0.0 copy-start.7
  237.0 0.9 fusion.1
  238.0 3.1 fusion.3
  241.1 3.9 %fusion.16 = f32[8,128,256]{2,1,0:T(8,128)S(1)} fusion(bf16[8,2048,128]{2,1,0:T(8,128)(2,1)} %fusion.3, bf16[2048,512]{1,0:T(8,128)(2,1)} %all-gather.2.cloned.1.call-done), kind=kOutput, calls=%fused_computation.21 | convolution fusion | flops 1073741824 | bytes 6291456 | tf_op jit(solution)/shard_map/ukc,kf->ucf/dot_general | solution.py:111
  245.0 8.8 %convert_bitcast_fusion.1 = bf16[2048,8,128]{0,2,1:T(8,128)(2,1)} fusion(bf16[256,2048,1]{1,0,2:T(8,128)(2,1)S(1)} %copy-done.2, bf16[8,2048,128]{2,1,0:T(8,128)(2,1)} %fusion.3, bf16[2048,512]{1,0:T(8,128)(2,1)} %all-gather.2.cloned.1.call-done, f32[8,128,256]{2,1,0:T(8,128)S(1)} %fusion.16), kind=kOutput, calls=%fused_computation.7 | convolution fusion | flops 2151153664 | bytes 11534336 | tf_op jit(solution)/shard_map/ucf,fk->kuc/dot_general | solution.py:116
  253.8 6.8 %copy.69 = bf16[2048,8,128]{2,1,0:T(8,128)(2,1)} copy(bf16[2048,8,128]{0,2,1:T(8,128)(2,1)} %convert_bitcast_fusion.1) | data formatting | bytes 8388608 | tf_op jit(solution)/shard_map/convert_element_type | solution.py:116
  260.6 2.5 copy.70
  263.1 8.2 %all_to_all.61 = bf16[2,16,64,8,128]{4,3,2,1,0:T(8,128)(2,1)} all-to-all(bf16[2,16,64,8,128]{4,3,2,1,0:T(8,128)(2,1)S(1)} %copy.70), channel_id=1, replica_groups=mesh['dp'=8,'mp_0'=4,'mp_1'=4,'mp_2'=2] {'mp_2'}, dimensions={0} | all-to-all | bytes 8388608 | tf_op jit(solution)/shard_map/all_to_all | solution.py:63
  271.2 3.3 %reduce_sum.64 = bf16[16,64,8,128]{3,2,1,0:T(8,128)(2,1)S(1)} reduce(bf16[2,16,64,8,128]{4,3,2,1,0:T(8,128)(2,1)} %all_to_all.61, bf16[]{:T(256)} %constant.18.clone.1), dimensions={0}, to_apply=%region_5.6 | reduce | flops 1048576 | bytes 6291458 | tf_op jit(solution)/shard_map/reduce_sum | solution.py:64
  274.6 31.5 %all_to_all.62 = bf16[16,64,8,128]{3,2,1,0:T(8,128)(2,1)} all-to-all(bf16[16,64,8,128]{3,2,1,0:T(8,128)(2,1)S(1)} %reduce_sum.64), channel_id=1, replica_groups=mesh['dp'=8,'mp_0'=4,'mp_1'=4,'mp_2'=2] {'mp_0','mp_1'}, dimensions={0} | all-to-all | bytes 4194304 | tf_op jit(solution)/shard_map/all_to_all | solution.py:71
  306.0 1.9 reduce_sum.65
  307.9 0.7 copy.71
  308.6 0.0 copy-done.1
  (8 shorter events, 0.0 us)
Async XLA Ops:
  6.5 47.4 %copy-start = (bf16[8,64,1024]{2,1,0:T(8,128)(2,1)S(1)}, bf16[8,64,1024]{2,1,0:T(8,128)(2,1)}, u32[]{:S(2)}) copy-start(bf16[8,64,1024]{2,1,0:T(8,128)(2,1)} %param.8) | copy-start | bytes 3145732
  51.0 2.9 copy-start.3
  80.0 7.8 %copy-start.8 = (s32[8]{0:T(128)S(1)}, s32[8]{0:T(128)}, u32[]{:S(2)}) copy-start(s32[8]{0:T(128)} %param.10) | copy-start | bytes 100
  81.6 38.5 %all-to-all-start.3 = ((f32[16,8,4,1024]{3,2,1,0:T(4,128)}), f32[16,8,4,1024]{3,2,1,0:T(4,128)S(1)}, u32[]{:S(2)}, u32[]{:S(2)}) async-start(f32[16,8,4,1024]{3,2,1,0:T(4,128)} %copy.60), calls=%async_computation.3 | async-start | bytes 4194304 | tf_op jit(solution)/shard_map/all_to_all | solution.py:45
  141.3 6.2 %copy-start.4 = (bf16[256,256]{1,0:T(8,128)(2,1)S(1)}, bf16[256,256]{1,0:T(8,128)(2,1)}, u32[]{:S(2)}) copy-start(bf16[256,256]{1,0:T(8,128)(2,1)} %param.15) | copy-start | bytes 393220
  148.6 37.6 %all-to-all-start.8 = ((bf16[8,256,256]{2,1,0:T(8,128)(2,1)}), bf16[8,256,256]{2,1,0:T(8,128)(2,1)}, u32[]{:S(2)}, u32[]{:S(2)}) async-start(bf16[8,256,256]{2,1,0:T(8,128)(2,1)} %broadcast_in_dim.53), calls=%async_computation.8 | async-start | bytes 2097152 | tf_op jit(solution)/shard_map/all_to_all | solution.py:14
  160.2 34.1 %copy-start.5 = (bf16[256,256]{1,0:T(8,128)(2,1)S(1)}, bf16[256,256]{1,0:T(8,128)(2,1)}, u32[]{:S(2)}) copy-start(bf16[256,256]{1,0:T(8,128)(2,1)} %param.14) | copy-start | bytes 393220
  160.2 34.1 %copy-start.6 = (bf16[256,256]{1,0:T(8,128)(2,1)S(1)}, bf16[256,256]{1,0:T(8,128)(2,1)}, u32[]{:S(2)}) copy-start(bf16[256,256]{1,0:T(8,128)(2,1)} %param.13) | copy-start | bytes 393220
  188.1 37.8 %all-to-all-start.6 = ((bf16[16,8,64,128]{3,2,1,0:T(8,128)(2,1)}), bf16[16,8,64,128]{3,2,1,0:T(8,128)(2,1)S(1)}, u32[]{:S(2)}, u32[]{:S(2)}) async-start(bf16[16,8,64,128]{3,2,1,0:T(8,128)(2,1)} %broadcast_in_dim.51), calls=%async_computation.6 | async-start | bytes 4194304 | tf_op jit(solution)/shard_map/all_to_all | solution.py:14
  194.2 46.9 %all-gather.2.cloned.1.call-start = ((), (), s32[]{:S(2)}) async-start(), calls=%async_computation.11 | async-start | bytes 2359296 | tf_op jit(solution)/shard_map/all_gather | solution.py:50
  237.0 1.0 copy-start.7
  241.1 3.9 %copy-start.2 = (bf16[256,2048,1]{1,0,2:T(8,128)(2,1)S(1)}, bf16[256,2048,1]{1,0,2:T(8,128)(2,1)}, u32[]{:S(2)}) copy-start(bf16[256,2048,1]{1,0,2:T(8,128)(2,1)} %reshape.70) | copy-start | bytes 3145732
  271.2 37.4 %copy-start.1 = (bf16[8,64,1024]{2,1,0:T(8,128)(2,1)S(1)}, bf16[8,64,1024]{2,1,0:T(8,128)(2,1)}, u32[]{:S(2)}) copy-start(bf16[8,64,1024]{2,1,0:T(8,128)(2,1)} %param.8) | copy-start | bytes 3145732
Sparse Core Ops, SparseCore 0:
  196.8 37.0 all-gather.1
where the time goes:
time: 318 us; the launch traced here: 315 us
  blocking collectives  120 us (38%)
  waiting for transfers between devices  86.1 us (27%)
  local copies, waits for them, and re-layouts  39.3 us (12%)
  starting transfers between devices  20.8 us (7%)
  matrix products  19.6 us (6%)
  other arithmetic  16.2 us (5%)
  between operations  13.6 us (4%)
    all_to_all x5, blocking collectives, copy_for_each(): return lax.all_to_all(copies, axis, split_axis=0, concat_axis=0, tiled=True)  72.1 us
    all_to_all x2, waiting for transfers between devices, copy_for_each(): return lax.all_to_all(copies, axis, split_axis=0, concat_axis=0, tiled=True)  53.8 us
    all_to_all x1, waiting for transfers between devices, sum_in_two_steps(): return jnp.sum(lax.all_to_all(own, far, 0, 0, tiled=True), axis=0)  32.2 us
    all_to_all x1, blocking collectives, sum_in_two_steps_2(): lax.all_to_all(own.astype(jnp.bfloat16), far, 0, 0, tiled=True)  31.5 us
    all_to_all x2, starting transfers between devices, copy_for_each(): return lax.all_to_all(copies, axis, split_axis=0, concat_axis=0, tiled=True)  14.5 us
    dot_general x1, matrix products, shards(): jnp.einsum('ucf,fk->kuc', hidden, down_full, preferred_element_type=jnp.f...  8.82 us
    all_to_all x1, blocking collectives, sent_and_summed(): lax.all_to_all(pieces, axis, split_axis=0, concat_axis=0, tiled=True)  8.17 us
    all_to_all x1, blocking collectives, sent_and_summed_2(): lax.all_to_all(pieces, axis, split_axis=0, concat_axis=0, tiled=True)  8.17 us
  transfers between devices with their start and end apart: 4, of which 3 were waited for; matrix products, arithmetic and copies ran while one was open for 5% of the time, Pallas kernels for 0%

commit v1 on v0

v1 whole, which is shorter than its diff:
```python
import math

import jax
import jax.numpy as jnp
from jax import lax
from jax.experimental import pallas as pl
from jax.experimental.pallas import tpu as pltpu
from jax.sharding import Mesh
from jax.sharding import PartitionSpec as P

MP = ("mp_0", "mp_1", "mp_2")
MESH = pl.DeviceIdType.MESH
BF = jnp.bfloat16
F32 = jnp.float32
USERS_HERE = 8
CANDS = 128
WIDTH = 2048
BEHAVIORS = 1024
TOKENS = USERS_HERE * CANDS
FEATS = 64
UNITS = 256
N_SEMS = 180


class Torus:
    def __init__(self, send_sem, recv_sem):
        self.z = lax.axis_index("dp")
        self.y = lax.axis_index("mp_0")
        self.x = lax.axis_index("mp_1")
        self.c = lax.axis_index("mp_2")
        self.a = self.x + self.c * (self.y - self.x)
        self.b = self.y + self.c * (self.x - self.y)
        self.send_sem, self.recv_sem = send_sem, recv_sem
        self.copies = []

    def dev_a(self, d):
        c = self.c
        return (self.z, lax.rem(self.y + c * d + 4, 4), lax.rem(self.x + (1 - c) * d + 4, 4), c)

    def dev_b(self, d):
        c = self.c
        return (self.z, lax.rem(self.y + (1 - c) * d + 4, 4), lax.rem(self.x + c * d + 4, 4), c)

    def dev_z(self, d):
        return (lax.rem(self.z + d + 8, 8), self.y, self.x, self.c)

    def partner(self):
        return (self.z, self.y, self.x, 1 - self.c)

    def send(self, src, dst, dev):
        i = len(self.copies)
        copy = pltpu.make_async_remote_copy(
            src_ref=src,
            dst_ref=dst,
            send_sem=self.send_sem.at[i],
            recv_sem=self.recv_sem.at[i],
            device_id=dev,
            device_id_type=MESH,
        )
        copy.start()
        self.copies.append(copy)
        return copy

    def finish(self):
        for copy in self.copies:
            copy.wait_send()

    def barrier(self):
        sem = pltpu.get_barrier_semaphore()
        peers = [
            self.dev_a(1),
            self.dev_a(-1),
            self.dev_b(1),
            self.dev_b(-1),
            self.dev_z(1),
            self.dev_z(-1),
            self.partner(),
        ]
        for dev in peers:
            pl.semaphore_signal(sem, inc=1, device_id=dev, device_id_type=MESH)
        pl.semaphore_wait(sem, len(peers))


def all_gather(t, slot, half):
    def at(da, db):
        return lax.rem(t.a + da + 4, 4), lax.rem(t.b + db + 4, 4)

    def whole(da, db, dev):
        ref = slot(*at(da, db))
        return t.send(ref, ref, dev)

    def part(da, db, h, dev):
        ref = half(*at(da, db), h)
        return t.send(ref, ref, dev)

    ap, am, bp, bm = t.dev_a(1), t.dev_a(-1), t.dev_b(1), t.dev_b(-1)
    twin = t.partner()
    twins = []
    first_p = whole(0, 0, ap)
    first_m = whole(0, 0, am)
    from_m, from_p = {}, {}
    from_m[0] = whole(0, 0, bp)
    from_p[0] = whole(0, 0, bm)
    twins.append(whole(0, 0, twin))
    first_p.wait_recv()
    far_0 = part(-1, 0, 0, ap)
    from_m[-1] = whole(-1, 0, bp)
    from_p[-1] = whole(-1, 0, bm)
    twins.append(whole(-1, 0, twin))
    first_m.wait_recv()
    far_1 = part(1, 0, 1, am)
    from_m[1] = whole(1, 0, bp)
    from_p[1] = whole(1, 0, bm)
    twins.append(whole(1, 0, twin))
    ends = {}

    def pass_on(q):
        from_m[q].wait_recv()
        e0 = part(q, -1, 0, bp)
        twins.append(whole(q, -1, twin))
        from_p[q].wait_recv()
        e1 = part(q, 1, 1, bm)
        twins.append(whole(q, 1, twin))
        ends[q] = (e0, e1)

    pass_on(0)
    far_0.wait_recv()
    far_1.wait_recv()
    from_m[2] = whole(2, 0, bp)
    from_p[2] = whole(2, 0, bm)
    twins.append(whole(2, 0, twin))
    for q in (-1, 1, 2):
        pass_on(q)
    for q in (0, -1, 1, 2):
        for e in ends[q]:
            e.wait_recv()
        twins.append(whole(q, 2, twin))
    for copy in twins:
        copy.wait_recv()


def ring_sum(t, p, plus, minus, terms, tx, rx):
    def g(d):
        return lax.rem(p + d + 4, 4)

    def emit(i, value, dev):
        tx[i] = value.astype(BF)
        return t.send(tx.at[i], rx.at[i], dev)

    c0 = emit(0, terms[g(2), 0], plus)
    c1 = emit(1, terms[g(2), 1], minus)
    c2 = emit(2, terms[g(1), 1], plus)
    c3 = emit(3, terms[g(-1), 0], minus)
    c0.wait_recv()
    c4 = emit(4, terms[g(1), 0] + rx[0].astype(F32), plus)
    c1.wait_recv()
    c5 = emit(5, terms[g(-1), 1] + rx[1].astype(F32), minus)
    c3.wait_recv()
    c2.wait_recv()
    c4.wait_recv()
    low = terms[p, 0] + rx[4].astype(F32) + rx[3].astype(F32)
    c5.wait_recv()
    high = terms[p, 1] + rx[2].astype(F32) + rx[5].astype(F32)
    return low, high


def reduce_scatter(t, term, twin_tx, twin_rx, terms, tx, rx, terms_2, tx_2, rx_2):
    other = 1 - t.c
    twins = []
    for d in (2, 1, -1, 0):
        g = lax.rem(t.a + d + 4, 4)
        twin_tx[g] = term(other, g).astype(BF)
        twins.append(t.send(twin_tx.at[g], twin_rx.at[g], t.partner()))
    rows = terms.shape[2]
    order = [lax.rem(t.b + d + 4, 4) for d in (2, 1, -1, 0)]
    for g in order:
        own = term(t.c, g)
        terms[g, 0] = own[:rows]
        terms[g, 1] = own[rows:]
    for copy, g in zip(twins, order):
        copy.wait_recv()
        terms[g, 0] += twin_rx[g, :rows].astype(F32)
        terms[g, 1] += twin_rx[g, rows:].astype(F32)
    low, high = ring_sum(t, t.b, t.dev_b(1), t.dev_b(-1), terms, tx, rx)
    n = terms_2.shape[2]
    for i, part in enumerate((low, high)):
        for j in range(2):
            for h in range(2):
                at = (2 * j + h) * n
                terms_2[2 * i + j, h] = part[at : at + n]
    return ring_sum(t, t.a, t.dev_a(1), t.dev_a(-1), terms_2, tx_2, rx_2)


def dot(a, b, dims=((1,), (0,))):
    return lax.dot_general(a, b, (dims, ((), ())), preferred_element_type=F32)


def kernel(
    cand,
    behaviors,
    lengths,
    bilinear,
    gain,
    w_gate,
    w_up,
    w_down,
    out,
    weights,
    cands,
    query,
    twin_tx,
    twin_rx,
    terms,
    tx,
    rx,
    terms_2,
    tx_2,
    rx_2,
    probs,
    pooled,
    hidden,
    out_twin_tx,
    out_twin_rx,
    out_terms,
    out_tx,
    out_rx,
    out_terms_2,
    out_tx_2,
    out_rx_2,
    send_sem,
    recv_sem,
):
    t = Torus(send_sem, recv_sem)
    t.barrier()
    mine = (t.y * 4 + t.x) * 2 + t.c

    own_gain = gain[pl.ds(t.z, 1), :]
    for i, w in enumerate((w_gate, w_up)):
        weights[t.z, pl.ds(i * UNITS, UNITS), :] = (w[...].astype(F32).T * own_gain).astype(BF)
    weights[t.z, pl.ds(2 * UNITS, UNITS), :] = w_down[...].astype(F32).T.astype(BF)

    def zat(d):
        return lax.rem(t.z + d + 8, 8)

    def pass_weights(d):
        up = t.send(weights.at[zat(1 - d)], weights.at[zat(1 - d)], t.dev_z(1))
        down = t.send(weights.at[zat(d - 1)], weights.at[zat(d - 1)], t.dev_z(-1))
        return up, down

    def feature_slot(buf):
        def chip(a, b):
            y = b + t.c * (a - b)
            x = a + t.c * (b - a)
            return (y * 4 + x) * 2 + t.c

        return (
            lambda a, b: buf.at[chip(a, b)],
            lambda a, b, h: buf.at[chip(a, b), pl.ds(h * (FEATS // 2), FEATS // 2), :],
        )

    for u in range(USERS_HERE):
        cands[mine, :, pl.ds(u * CANDS, CANDS)] = cand[u]
    w_hop = pass_weights(1)
    all_gather(t, *feature_slot(cands))

    q = dot(bilinear[...], cands[...].reshape(WIDTH, TOKENS)).astype(BF)
    for u in range(USERS_HERE):
        query[u] = q[:, u * CANDS : (u + 1) * CANDS]
    for copy in w_hop:
        copy.wait_recv()
    w_hop = pass_weights(2)

    def scores(core, group):
        u = core * 4 + group
        return dot(query[u], behaviors[u], ((0,), (0,)))

    low, high = reduce_scatter(
        t, scores, twin_tx, twin_rx, terms, tx, rx, terms_2, tx_2, rx_2
    )
    for copy in w_hop:
        copy.wait_recv()
    w_hop = pass_weights(3)
    length = lengths[t.c * 4 + t.b]
    block = t.c * 16 + t.b * 4 + t.a
    for i, part in enumerate((low, high)):
        s = part * (1.0 / math.sqrt(WIDTH))
        live = lax.broadcasted_iota(jnp.int32, s.shape, 1) < length
        s = jnp.where(live, s, -1e30)
        e = jnp.where(live, jnp.exp(s - jnp.max(s, axis=1, keepdims=True)), 0.0)
        e = e / jnp.sum(e, axis=1, keepdims=True)
        n = s.shape[0]
        probs[block, pl.ds(i * n, n), :] = e.astype(BF)

    all_gather(
        t,
        lambda a, b: probs.at[t.c * 16 + b * 4 + a],
        lambda a, b, h: probs.at[t.c * 16 + b * 4 + a, pl.ds(h * 16, 16), :],
    )
    for copy in w_hop:
        copy.wait_recv()
    far_w = zat(4)
    last_up = t.send(
        weights.at[zat(-3), pl.ds(0, 384)], weights.at[zat(-3), pl.ds(0, 384)], t.dev_z(1)
    )
    last_down = t.send(
        weights.at[zat(3), pl.ds(384, 384)], weights.at[zat(3), pl.ds(384, 384)], t.dev_z(-1)
    )
    for u in range(USERS_HERE):
        p = probs[pl.ds(4 * u, 4)].reshape(CANDS, BEHAVIORS)
        pooled[mine, :, pl.ds(u * CANDS, CANDS)] = dot(
            behaviors[u], p, ((1,), (1,))
        ).astype(BF)
    all_gather(t, *feature_slot(pooled))
    last_up.wait_recv()
    last_down.wait_recv()

    n = 256
    for i in range(TOKENS // n):
        lanes = pl.ds(i * n, n)
        acc = jnp.zeros((2 * UNITS, n), F32)
        squares = jnp.zeros((1, n), F32)
        for k in range(8):
            x = pooled[pl.ds(4 * k, 4), :, lanes].reshape(256, n)
            acc += dot(weights[k, pl.ds(0, 2 * UNITS), :], x)
            v = x.astype(F32)
            squares += jnp.sum(v * v, axis=0, keepdims=True)
        acc = acc * lax.rsqrt(squares * (1.0 / WIDTH) + 1e-6)
        gate, upward = acc[:UNITS], acc[UNITS:]
        hidden[:, lanes] = (gate / (1.0 + jnp.exp(-gate)) * upward).astype(BF)

    def outputs(core, group):
        parts = []
        for i in range(4):
            y = group + core * (i - group)
            x = i + core * (group - i)
            m = (y * 4 + x) * 2 + core
            at = 2 * UNITS + lax.rem(m, 4) * FEATS
            parts.append(weights[m // 4, pl.ds(pl.multiple_of(at, FEATS), FEATS), :])
        return dot(jnp.concatenate(parts, axis=0), hidden[...])

    low, high = reduce_scatter(
        t,
        outputs,
        out_twin_tx,
        out_twin_rx,
        out_terms,
        out_tx,
        out_rx,
        out_terms_2,
        out_tx_2,
        out_rx_2,
    )
    n = FEATS // 2
    for u in range(USERS_HERE):
        out[u, pl.ds(0, n), :] = low[:, u * CANDS : (u + 1) * CANDS].astype(BF)
        out[u, pl.ds(n, n), :] = high[:, u * CANDS : (u + 1) * CANDS].astype(BF)
    t.finish()


def shards(behaviors, candidates, lengths, bilinear, norm_gain, w_gate, w_up, w_down):
    vmem = pl.BlockSpec(memory_space=pltpu.VMEM)
    smem = pl.BlockSpec(memory_space=pltpu.SMEM)
    return pl.pallas_call(
        kernel,
        out_shape=jax.ShapeDtypeStruct(candidates.shape, BF),
        in_specs=[vmem, vmem, smem, vmem, vmem, vmem, vmem, vmem],
        out_specs=vmem,
        scratch_shapes=[
            pltpu.VMEM((8, 3 * UNITS, UNITS), BF),
            pltpu.VMEM((32, FEATS, TOKENS), BF),
            pltpu.VMEM((USERS_HERE, FEATS, CANDS), BF),
            pltpu.VMEM((4, CANDS, BEHAVIORS), BF),
            pltpu.VMEM((4, CANDS, BEHAVIORS), BF),
            pltpu.VMEM((4, 2, 64, BEHAVIORS), F32),
            pltpu.VMEM((6, 64, BEHAVIORS), BF),
            pltpu.VMEM((6, 64, BEHAVIORS), BF),
            pltpu.VMEM((4, 2, 16, BEHAVIORS), F32),
            pltpu.VMEM((6, 16, BEHAVIORS), BF),
            pltpu.VMEM((6, 16, BEHAVIORS), BF),
            pltpu.VMEM((32, 32, BEHAVIORS), BF),
            pltpu.VMEM((32, FEATS, TOKENS), BF),
            pltpu.VMEM((UNITS, TOKENS), BF),
            pltpu.VMEM((4, 256, TOKENS), BF),
            pltpu.VMEM((4, 256, TOKENS), BF),
            pltpu.VMEM((4, 2, 128, TOKENS), F32),
            pltpu.VMEM((6, 128, TOKENS), BF),
            pltpu.VMEM((6, 128, TOKENS), BF),
            pltpu.VMEM((4, 2, 32, TOKENS), F32),
            pltpu.VMEM((6, 32, TOKENS), BF),
            pltpu.VMEM((6, 32, TOKENS), BF),
            pltpu.SemaphoreType.DMA((N_SEMS,)),
            pltpu.SemaphoreType.DMA((N_SEMS,)),
        ],
        compiler_params=pltpu.CompilerParams(
            collective_id=0, has_side_effects=True, vmem_limit_bytes=56 * 1024 * 1024
        ),
    )(
        candidates,
        behaviors,
        lengths,
        bilinear,
        norm_gain.reshape(8, 256),
        w_gate,
        w_up,
        w_down,
    )


def solution(mesh):
    finer = Mesh(mesh.devices.reshape(mesh.shape["dp"], 4, 4, 2), ("dp", "mp_0", "mp_1", "mp_2"))
    return jax.shard_map(
        shards,
        mesh=finer,
        in_specs=(
            P("dp", MP, None),
            P("dp", MP, None),
            P("dp"),
            P(MP, None),
            P(),
            P("dp", MP),
            P("dp", MP),
            P(MP, "dp"),
        ),
        out_specs=P("dp", MP, None),
        check_vma=False,
    )
```

time: 318 us -> 116 us (0.36)
  blocking collectives: 120 us -> 0 us
  Pallas kernels: 0 us -> 112 us
  waiting for transfers between devices: 86.1 us -> 0 us
  local copies, waits for them, and re-layouts: 39.3 us -> 2.87 us
  starting transfers between devices: 20.8 us -> 0 us
  matrix products: 19.6 us -> 0 us
  other arithmetic: 16.2 us -> 0 us
  between operations: 13.6 us -> 0.01 us
    all_to_all x8 -> x0, blocking collectives: 120 us -> none  [the longest x5 72.1 us: copy_for_each(): return lax.all_to_all(copies, axis, split_axis=0, concat_axis=0, tiled=True)]
    pallas_call x0 -> x1, Pallas kernels: none -> 112 us  [shards(): pl.pallas_call(kernel, out_shape=jax.ShapeDtypeStruct(candidates.shape, B...]
    all_to_all x3 -> x0, waiting for transfers between devices: 86.1 us -> none  [the longest x2 53.8 us: copy_for_each(): return lax.all_to_all(copies, axis, split_axis=0, concat_axis=0, tiled=True)]
    all_to_all x3 -> x0, starting transfers between devices: 20.7 us -> none  [the longest x2 14.5 us: copy_for_each(): return lax.all_to_all(copies, axis, split_axis=0, concat_axis=0, tiled=True)]
    dot_general x4 -> x0, matrix products: 19.6 us -> none  [the longest x1 8.82 us: shards(): jnp.einsum('ucf,fk->kuc', hidden, down_full, preferred_element_type=jnp.f...]
    reduce_sum x5 -> x0, other arithmetic: 10.9 us -> none  [the longest x1 4.23 us: sent_and_summed(): return arrived.sum(axis=0)]
    transpose x4 -> x0, local copies, waits for them, and re-layouts: 9.87 us -> none  [the longest x2 5.17 us: cut_along(): return jnp.moveaxis(pieces, dim, 0)]
    convert_element_type x3 -> x0, local copies, waits for them, and re-layouts: 9.13 us -> none  [the longest x1 6.79 us: shards(): jnp.einsum('ucf,fk->kuc', hidden, down_full, preferred_element_type=jnp.f...]
  transfers between devices with their start and end apart: 4 -> 0, of which waited for: 3 -> 0; matrix products, arithmetic and copies ran while one was open for 5% -> 0% of each run, Pallas kernels for 0% -> 0%
where the time goes in v1:
time: 116 us; the launch traced here: 115 us
  Pallas kernels  112 us (97%)
  local copies, waits for them, and re-layouts  2.87 us (2%)
    pallas_call x1, Pallas kernels, shards(): pl.pallas_call(kernel, out_shape=jax.ShapeDtypeStruct(candidates.shape, B...  112 us

profile of v1, /device:TPU:8, one launch (start us, length us, event | category | flops | bytes accessed | tf_op | source)
XLA Modules:
  0.0 114.7 jit_solution(1941187315826260805)
XLA Ops:
  0.0 1.3 %reshape.3.gain = f32[8,256]{1,0:T(8,128)} reshape(f32[2048]{0:T(1024)} %param.12) | data formatting | bytes 16384 | tf_op jit(solution)/shard_map/reshape | solution.py:402
  1.3 111.9 %shard_map.82 = bf16[8,64,128]{2,1,0:T(8,128)(2,1)} custom-call(bf16[8,64,128]{2,1,0:T(8,128)(2,1)} %cand.1, bf16[8,64,1024]{2,1,0:T(8,128)(2,1)} %behaviors.1, s32[8]{0:T(128)} %lengths.1, bf16[64,2048]{1,0:T(8,128)(2,1)} %bilinear.1, f32[8,256]{1,0:T(8,128)} %reshape.3.gain, bf16[256,256]{1,0:T(8,128)(2,1)} %w_gate.1, bf16[256,256]{1,0:T(8,128)(2,1)} %w_up.1, ...), custom_call_target="tpu_custom_call" | custom-call | tf_op jit(solution)/shard_map/pallas_call | solution.py:363
  113.2 1.6 %copy.10 = bf16[8,64,128]{2,1,0:T(8,128)(2,1)} copy(bf16[8,64,128]{2,1,0:T(8,128)(2,1)} %shard_map.82) | data formatting | bytes 262144

commit v2 on v0

v2 whole, which is shorter than its diff:
```python
import math

import jax
import jax.numpy as jnp
from jax import lax
from jax.experimental import pallas as pl
from jax.experimental.pallas import tpu as pltpu
from jax.sharding import Mesh
from jax.sharding import PartitionSpec as P

MP = ("mp_0", "mp_1", "mp_2")
MESH = pl.DeviceIdType.MESH
BF = jnp.bfloat16
F32 = jnp.float32
USERS_HERE = 8
CANDS = 128
WIDTH = 2048
BEHAVIORS = 1024
CHUNKS = 2
CHUNK_USERS = USERS_HERE // CHUNKS
TOKENS = CHUNK_USERS * CANDS
QUARTER = BEHAVIORS // 4
FEATURES = WIDTH // 4
ROWS = CANDS // CHUNKS
OTHERS = sorted(
    ((dy, dx, dc) for dy in range(4) for dx in range(4) for dc in range(2) if dy + dx + dc),
    key=lambda d: (-min(d[0], 4 - d[0]) - min(d[1], 4 - d[1]), d),
)
LEAD = 0
LAST_HOP = 9
TICK = 2
FEATS = 64
UNITS = 256
N_SEMS = 320


class Torus:
    def __init__(self, send_sem, recv_sem):
        self.z = lax.axis_index("dp")
        self.y = lax.axis_index("mp_0")
        self.x = lax.axis_index("mp_1")
        self.c = lax.axis_index("mp_2")
        self.a = self.x + self.c * (self.y - self.x)
        self.b = self.y + self.c * (self.x - self.y)
        self.me = (self.y * 4 + self.x) * 2 + self.c
        self.user, self.quarter = owned(self.y, self.x, self.c)
        self.send_sem, self.recv_sem = send_sem, recv_sem
        self.copies = []

    def chip(self, a, b):
        return b + self.c * (a - b), a + self.c * (b - a)

    def shifted(self, dy, dx, dc):
        core = 1 - self.c if dc else self.c
        return lax.rem(self.y + dy, 4), lax.rem(self.x + dx, 4), core

    def dev_a(self, d):
        c = self.c
        return (self.z, lax.rem(self.y + c * d + 4, 4), lax.rem(self.x + (1 - c) * d + 4, 4), c)

    def dev_b(self, d):
        c = self.c
        return (self.z, lax.rem(self.y + (1 - c) * d + 4, 4), lax.rem(self.x + c * d + 4, 4), c)

    def dev_z(self, d):
        return (lax.rem(self.z + d + 8, 8), self.y, self.x, self.c)

    def partner(self):
        return (self.z, self.y, self.x, 1 - self.c)

    def send(self, src, dst, dev):
        i = len(self.copies)
        copy = pltpu.make_async_remote_copy(
            src_ref=src,
            dst_ref=dst,
            send_sem=self.send_sem.at[i],
            recv_sem=self.recv_sem.at[i],
            device_id=dev,
            device_id_type=MESH,
        )
        copy.start()
        self.copies.append(copy)
        return copy

    def finish(self):
        for copy in self.copies:
            copy.wait_send()

    def barrier(self):
        sem = pltpu.get_barrier_semaphore()
        peers = [self.dev_z(1), self.dev_z(-1)]
        peers += [(self.z, *self.shifted(*d)) for d in OTHERS]
        for dev in peers:
            pl.semaphore_signal(sem, inc=1, device_id=dev, device_id_type=MESH)
        pl.semaphore_wait(sem, len(peers))


def owned(y, x, core):
    return y * 2 + x // 2, lax.rem(x, 2) * 2 + core


def all_gather(t, slot):
    def whole(da, db, dev):
        ref = slot(lax.rem(t.a + da + 4, 4), lax.rem(t.b + db + 4, 4))
        return t.send(ref, ref, dev)

    twin = t.partner()
    row = {d: whole(0, 0, t.dev_a(d)) for d in (2, 1, -1)}
    column = {(0, d): whole(0, 0, t.dev_b(d)) for d in (2, 1, -1)}
    twins = [whole(0, 0, twin)]
    for q in (-1, 1, 2):
        yield
        row[q].wait_recv()
        for d in (2, 1, -1):
            column[-q, d] = whole(-q, 0, t.dev_b(d))
        twins.append(whole(-q, 0, twin))
    for (q, d), copy in column.items():
        yield
        copy.wait_recv()
        twins.append(whole(q, -d, twin))
    yield
    for copy in twins:
        copy.wait_recv()


def ring_sum(t, p, dev, terms, tx, rx):
    copies = []
    for i, d in enumerate((2, 1, -1)):
        tx[i] = terms[lax.rem(p + d + 4, 4)].astype(tx.dtype)
        copies.append(t.send(tx.at[i], rx.at[i], dev(d)))
    total = terms[p]
    for i in (1, 2, 0):
        yield
        copies[i].wait_recv()
        total += rx[i].astype(F32)
    return total


def reduce_scatter(t, term, twin_tx, twin_rx, terms, tx, rx, terms_2, tx_2, rx_2):
    other = 1 - t.c
    twins = []
    for d in (2, 1, -1, 0):
        g = lax.rem(t.a + d + 4, 4)
        twin_tx[g] = term(other, g).astype(twin_tx.dtype)
        twins.append(t.send(twin_tx.at[g], twin_rx.at[g], t.partner()))
    order = [lax.rem(t.b + d + 4, 4) for d in (2, 1, -1, 0)]
    for g in order:
        terms[g] = term(t.c, g)
    yield
    for copy, g in zip(twins, order):
        copy.wait_recv()
        terms[g] += twin_rx[g].astype(F32)
    total = yield from ring_sum(t, t.b, t.dev_b, terms, tx, rx)
    n = terms_2.shape[1]
    for i in range(4):
        terms_2[i] = total[i * n : (i + 1) * n]
    return (yield from ring_sum(t, t.a, t.dev_a, terms_2, tx_2, rx_2))


def dot(a, b, dims=((1,), (0,))):
    return lax.dot_general(a, b, (dims, ((), ())), preferred_element_type=F32)


class Weights:
    def __init__(self, t, buf):
        self.t, self.buf, self.hops, self.pending, self.ticks = t, buf, 0, (), 0

    def at(self, d):
        return lax.rem(self.t.z + d + 8, 8)

    def wait(self):
        for copy in self.pending:
            copy.wait_recv()
        self.pending = ()

    def late_hop(self):
        self.ticks += 1
        if self.ticks == LAST_HOP:
            self.hop()

    def hop(self):
        self.wait()
        t, d = self.t, self.hops
        self.hops += 1
        up, down = self.buf.at[self.at(-d)], self.buf.at[self.at(d)]
        if d == 3:
            n = self.buf.shape[1] // 2
            up = self.buf.at[self.at(-d), pl.ds(0, n)]
            down = self.buf.at[self.at(d), pl.ds(n, n)]
        self.pending = (t.send(up, up, t.dev_z(1)), t.send(down, down, t.dev_z(-1)))


def together(chains, tick=None, lead=0):
    chains = list(chains)
    ended = object()
    for _ in range(lead):
        next(chains[0])
    while chains:
        for one in list(chains):
            if next(one, ended) is ended:
                chains.remove(one)
        if tick is not None:
            tick()


def attend(t, mem, w):
    u = t.user
    copies = []
    for dy, dx, dc in OTHERS:
        if dc == 0:
            y, x, c = t.shifted(dy, dx, dc)
            copies.append((dy, dx, t.send(mem.query.at[owned(y, x, c)[0]], mem.keys.at[t.me], (t.z, y, x, c))))
    mem.keys[t.me] = mem.query[u]
    twins = [t.send(mem.keys.at[t.me], mem.keys.at[t.me], t.partner())]
    w.hop()
    for dy, dx, copy in reversed(copies):
        copy.wait_recv()
        y, x = lax.rem(t.y - dy + 4, 4), lax.rem(t.x - dx + 4, 4)
        ref = mem.keys.at[(y * 4 + x) * 2 + t.c]
        twins.append(t.send(ref, ref, t.partner()))
    for copy in mem.moved:
        copy.wait_recv()
    mem.own_behaviors.wait()
    for copy in twins:
        copy.wait_recv()
    behaviors = mem.behaviors[...].reshape(WIDTH, QUARTER)
    s = dot(mem.keys[...].reshape(WIDTH, CANDS), behaviors, ((0,), (0,)))
    s = s * (1.0 / math.sqrt(WIDTH))
    at = lax.broadcasted_iota(jnp.int32, s.shape, 1) + t.quarter * QUARTER
    live = at < mem.lengths[u]
    s = jnp.where(live, s, -1e30)
    highest = jnp.max(s, axis=1, keepdims=True)
    e = jnp.where(live, jnp.exp(s - highest), 0.0)
    total = jnp.sum(e, axis=1, keepdims=True)
    some = total > 0.0
    total = jnp.where(some, total, 1.0)
    level = jnp.where(some, highest + jnp.log(total), -1e30)
    level = jnp.broadcast_to(level, (CANDS, 128))
    mem.levels[...] = level
    mem.level_tx[...] = level.T[:8]
    mem.level_copies = [
        t.send(mem.level_tx, mem.level_rx.at[i], dev) for i, (dev, _) in enumerate(owners(t))
    ]
    p = (e / total).astype(BF)
    for i in range(4):
        mem.means[i] = dot(p, mem.behaviors[pl.ds(8 * i, 8)].reshape(FEATURES, QUARTER), ((1,), (1,)))


def owners(t):
    x = t.x + 1 - 2 * lax.rem(t.x, 2)
    result = []
    for xx, c in ((x, 1 - t.c), (x, t.c), (t.x, 1 - t.c)):
        result.append(((t.z, t.y, xx, c), owned(t.y, xx, c)[1]))
    return result


def chain(t, h, mem, w):
    rows = pl.ds(h * ROWS, ROWS)
    copies = []
    for i, (dev, quarter) in enumerate(owners(t)):
        mem.mean_tx[h, i] = mem.means[quarter, rows, :].astype(BF)
        copies.append(t.send(mem.mean_tx.at[h, i], mem.mean_rx.at[h, i], dev))
    yield
    if h == 0:
        for copy in mem.level_copies:
            copy.wait_recv()
        levels = [mem.levels[...]]
        levels += [jnp.broadcast_to(mem.level_rx[i][:1], (128, CANDS)).T for i in range(3)]
        top = jnp.maximum(jnp.maximum(levels[0], levels[1]), jnp.maximum(levels[2], levels[3]))
        shares = [jnp.exp(level - top) for level in levels]
        scale = 1.0 / (shares[0] + shares[1] + shares[2] + shares[3])
        for i in range(4):
            mem.shares[i] = shares[i] * scale

    def share(i):
        return jnp.concatenate([mem.shares[i, rows, :]] * (FEATURES // 128), axis=1)

    total = mem.means[t.quarter, rows, :] * share(0)
    for i in (2, 1, 0):
        copies[i].wait_recv()
        total += mem.mean_rx[h, i].astype(F32) * share(i + 1)
    mem.pooled[h, t.quarter, t.user] = total.astype(BF)

    def pooled_slot(a, b):
        user, quarter = owned(*t.chip(a, b), t.c)
        return mem.pooled.at[h, quarter, user]

    yield from all_gather(t, pooled_slot)
    if h == 0:
        w.wait()

    n = 256
    for i in range(TOKENS // n):
        acc = jnp.zeros((n, 2 * UNITS), F32)
        squares = jnp.zeros((n, 1), F32)
        for k in range(4):
            x = mem.pooled[h, k, pl.ds(4 * i, 4)].reshape(n, FEATURES)
            acc += dot(x, mem.weights[pl.ds(2 * k, 2), :, pl.ds(0, 2 * UNITS)].reshape(FEATURES, 2 * UNITS))
            v = x.astype(F32)
            squares += jnp.sum(v * v, axis=1, keepdims=True)
        acc = acc * lax.rsqrt(squares * (1.0 / WIDTH) + 1e-6)
        gate, upward = acc[:, :UNITS], acc[:, UNITS:]
        value = gate / (1.0 + jnp.exp(-gate)) * upward
        mem.hidden[h, :, pl.ds(i * n, n)] = value.T.astype(BF)
    yield

    def outputs(core, group):
        parts = []
        for i in range(4):
            y = group + core * (i - group)
            x = i + core * (group - i)
            m = (y * 4 + x) * 2 + core
            at = pl.multiple_of(lax.rem(m, 4) * FEATS, FEATS)
            parts.append(mem.weights[m // 4, pl.ds(at, FEATS), pl.ds(2 * UNITS, UNITS)])
        return dot(jnp.concatenate(parts, axis=0), mem.hidden[h])

    total = yield from reduce_scatter(
        t,
        outputs,
        *(ref.at[h] for ref in mem.out_1),
        *(ref.at[h] for ref in mem.out_2),
    )
    mem.result[h] = total


class Memory:
    pass


def kernel(
    cand_in,
    behaviors_in,
    lengths,
    bilinear_in,
    gain,
    w_gate_in,
    w_up_in,
    w_down_in,
    out,
    behaviors,
    bilinear,
    raw_weights,
    weights,
    cands,
    query,
    keys,
    means,
    mean_tx,
    mean_rx,
    levels,
    level_tx,
    level_rx,
    shares,
    pooled,
    hidden,
    result,
    *rest,
):
    send_sem, recv_sem, in_sem = rest[-3:]
    t = Torus(send_sem, recv_sem)
    mem = Memory()
    mem.behaviors, mem.bilinear, mem.weights, mem.cands = behaviors, bilinear, weights, cands
    mem.query, mem.keys, mem.pooled, mem.hidden = query, keys, pooled, hidden
    mem.means, mem.mean_tx, mem.mean_rx, mem.shares = means, mean_tx, mean_rx, shares
    mem.levels, mem.level_tx, mem.level_rx = levels, level_tx, level_rx
    mem.lengths, mem.result = lengths, result
    mem.out_1, mem.out_2 = rest[0:5], rest[5:8]

    started = []

    def fetch(src, dst):
        copy = pltpu.make_async_copy(src, dst, in_sem.at[len(started)])
        copy.start()
        started.append(copy)
        return copy

    cand_copies = [
        fetch(
            cand_in.at[u],
            cands.at[u // CHUNK_USERS, t.me, :, pl.ds(u % CHUNK_USERS * CANDS, CANDS)],
        )
        for u in range(USERS_HERE)
    ]
    weight_copies = [
        fetch(w, raw_weights.at[i]) for i, w in enumerate((w_gate_in, w_up_in, w_down_in))
    ]
    bilinear_copy = fetch(bilinear_in, bilinear)

    def behaviors_of(y, x, core):
        user, quarter = owned(y, x, core)
        at = pl.multiple_of(quarter * QUARTER, QUARTER)
        return behaviors_in.at[user, :, pl.ds(at, QUARTER)]

    mem.own_behaviors = fetch(behaviors_of(t.y, t.x, t.c), behaviors.at[t.me])
    t.barrier()

    to_move = list(OTHERS)
    mem.moved = []

    def move_behaviors(count=TICK):
        for _ in range(min(count, len(to_move))):
            y, x, c = t.shifted(*to_move.pop(0))
            mem.moved.append(t.send(behaviors_of(y, x, c), behaviors.at[t.me], (t.z, y, x, c)))

    def cand_slot(h):
        def slot(a, b):
            y, x = t.chip(a, b)
            return cands.at[h, (y * 4 + x) * 2 + t.c]

        return slot

    w = Weights(t, weights)
    for copy in cand_copies:
        copy.wait()
    gathers = [all_gather(t, cand_slot(h)) for h in range(CHUNKS)]
    for one in gathers:
        next(one)
    move_behaviors()

    own_gain = jnp.broadcast_to(gain[pl.ds(t.z, 1), :], (128, UNITS)).T
    own_gain = jnp.concatenate([own_gain, own_gain], axis=1)
    for i in range(3):
        weight_copies[i].wait()
        v = raw_weights[i].astype(F32)
        v = v * own_gain if i < 2 else v.T
        weights[t.z, :, pl.ds(i * UNITS, UNITS)] = v.astype(BF)
    w.hop()

    together(gathers, move_behaviors)
    move_behaviors(len(to_move))
    bilinear_copy.wait()
    for h in range(CHUNKS):
        q = dot(bilinear[...], cands[h].reshape(WIDTH, TOKENS)).astype(BF)
        for u in range(CHUNK_USERS):
            query[h * CHUNK_USERS + u] = q[:, u * CANDS : (u + 1) * CANDS]
    attend(t, mem, w)
    w.hop()
    together([chain(t, h, mem, w) for h in range(CHUNKS)], w.late_hop, LEAD)
    for u in range(USERS_HERE):
        parts = [result[h, :, pl.ds(u // 2 * 128, 128)] for h in range(CHUNKS)]
        if u % 2 == 0:
            both = jnp.concatenate([part[:, :ROWS] for part in parts], axis=1)
        else:
            both = jnp.concatenate([part[:, ROWS:] for part in parts], axis=1)
        out[u] = both.astype(BF)
    t.finish()


def exchange_buffers(rows, piece, width):
    return (
        pltpu.VMEM((CHUNKS, 4, rows, width), BF),
        pltpu.VMEM((CHUNKS, 4, rows, width), BF),
        pltpu.VMEM((CHUNKS, 4, rows, width), F32),
        pltpu.VMEM((CHUNKS, 3, rows, width), BF),
        pltpu.VMEM((CHUNKS, 3, rows, width), BF),
        pltpu.VMEM((CHUNKS, 4, piece, width), F32),
        pltpu.VMEM((CHUNKS, 3, piece, width), BF),
        pltpu.VMEM((CHUNKS, 3, piece, width), BF),
    )


def shards(behaviors, candidates, lengths, bilinear, norm_gain, w_gate, w_up, w_down):
    vmem = pl.BlockSpec(memory_space=pltpu.VMEM)
    hbm = pl.BlockSpec(memory_space=pl.ANY)
    smem = pl.BlockSpec(memory_space=pltpu.SMEM)
    return pl.pallas_call(
        kernel,
        out_shape=jax.ShapeDtypeStruct(candidates.shape, BF),
        in_specs=[hbm, hbm, smem, hbm, vmem, hbm, hbm, hbm],
        out_specs=vmem,
        scratch_shapes=[
            pltpu.VMEM((32, FEATS, QUARTER), BF),
            pltpu.VMEM(bilinear.shape, BF),
            pltpu.VMEM((3, UNITS, UNITS), BF),
            pltpu.VMEM((8, UNITS, 3 * UNITS), BF),
            pltpu.VMEM((CHUNKS, 32, FEATS, TOKENS), BF),
            pltpu.VMEM((USERS_HERE, FEATS, CANDS), BF),
            pltpu.VMEM((32, FEATS, CANDS), BF),
            pltpu.VMEM((4, CANDS, FEATURES), F32),
            pltpu.VMEM((CHUNKS, 3, ROWS, FEATURES), BF),
            pltpu.VMEM((CHUNKS, 3, ROWS, FEATURES), BF),
            pltpu.VMEM((CANDS, 128), F32),
            pltpu.VMEM((8, CANDS), F32),
            pltpu.VMEM((3, 8, CANDS), F32),
            pltpu.VMEM((4, CANDS, 128), F32),
            pltpu.VMEM((CHUNKS, 4, USERS_HERE, ROWS, FEATURES), BF),
            pltpu.VMEM((CHUNKS, UNITS, TOKENS), BF),
            pltpu.VMEM((CHUNKS, FEATS, TOKENS), F32),
            *exchange_buffers(256, FEATS, TOKENS),
            pltpu.SemaphoreType.DMA((N_SEMS,)),
            pltpu.SemaphoreType.DMA((N_SEMS,)),
            pltpu.SemaphoreType.DMA((16,)),
        ],
        compiler_params=pltpu.CompilerParams(
            collective_id=0, has_side_effects=True, vmem_limit_bytes=56 * 1024 * 1024
        ),
    )(
        candidates,
        behaviors,
        lengths,
        bilinear,
        norm_gain.reshape(8, 256),
        w_gate,
        w_up,
        w_down,
    )


def solution(mesh):
    finer = Mesh(mesh.devices.reshape(mesh.shape["dp"], 4, 4, 2), ("dp", "mp_0", "mp_1", "mp_2"))
    return jax.shard_map(
        shards,
        mesh=finer,
        in_specs=(
            P("dp", MP, None),
            P("dp", MP, None),
            P("dp"),
            P(MP, None),
            P(),
            P("dp", MP),
            P("dp", MP),
            P(MP, "dp"),
        ),
        out_specs=P("dp", MP, None),
        check_vma=False,
    )
```

time: 318 us -> 112 us (0.35)
  blocking collectives: 120 us -> 0 us
  Pallas kernels: 0 us -> 108 us
  waiting for transfers between devices: 86.1 us -> 0 us
  local copies, waits for them, and re-layouts: 39.3 us -> 2.87 us
  starting transfers between devices: 20.8 us -> 0 us
  matrix products: 19.6 us -> 0 us
  other arithmetic: 16.2 us -> 0 us
  between operations: 13.6 us -> 0.01 us
    all_to_all x8 -> x0, blocking collectives: 120 us -> none  [the longest x5 72.1 us: copy_for_each(): return lax.all_to_all(copies, axis, split_axis=0, concat_axis=0, tiled=True)]
    pallas_call x0 -> x1, Pallas kernels: none -> 108 us  [shards(): pl.pallas_call(kernel, out_shape=jax.ShapeDtypeStruct(candidates.shape, B...]
    all_to_all x3 -> x0, waiting for transfers between devices: 86.1 us -> none  [the longest x2 53.8 us: copy_for_each(): return lax.all_to_all(copies, axis, split_axis=0, concat_axis=0, tiled=True)]
    all_to_all x3 -> x0, starting transfers between devices: 20.7 us -> none  [the longest x2 14.5 us: copy_for_each(): return lax.all_to_all(copies, axis, split_axis=0, concat_axis=0, tiled=True)]
    dot_general x4 -> x0, matrix products: 19.6 us -> none  [the longest x1 8.82 us: shards(): jnp.einsum('ucf,fk->kuc', hidden, down_full, preferred_element_type=jnp.f...]
    reduce_sum x5 -> x0, other arithmetic: 10.9 us -> none  [the longest x1 4.23 us: sent_and_summed(): return arrived.sum(axis=0)]
    transpose x4 -> x0, local copies, waits for them, and re-layouts: 9.87 us -> none  [the longest x2 5.17 us: cut_along(): return jnp.moveaxis(pieces, dim, 0)]
    convert_element_type x3 -> x0, local copies, waits for them, and re-layouts: 9.13 us -> none  [the longest x1 6.79 us: shards(): jnp.einsum('ucf,fk->kuc', hidden, down_full, preferred_element_type=jnp.f...]
  transfers between devices with their start and end apart: 4 -> 0, of which waited for: 3 -> 0; matrix products, arithmetic and copies ran while one was open for 5% -> 0% of each run, Pallas kernels for 0% -> 0%
where the time goes in v2:
time: 112 us; the launch traced here: 111 us
  Pallas kernels  108 us (96%)
  local copies, waits for them, and re-layouts  2.87 us (3%)
    pallas_call x1, Pallas kernels, shards(): pl.pallas_call(kernel, out_shape=jax.ShapeDtypeStruct(candidates.shape, B...  108 us

profile of v2, /device:TPU:8, one launch (start us, length us, event | category | flops | bytes accessed | tf_op | source)
XLA Modules:
  0.0 111.1 jit_solution(5621210782485416226)
XLA Ops:
  0.0 1.3 %reshape.3.gain = f32[8,256]{1,0:T(8,128)} reshape(f32[2048]{0:T(1024)} %param.12) | data formatting | bytes 16384 | tf_op jit(solution)/shard_map/reshape | solution.py:502
  1.3 108.2 %shard_map.82 = bf16[8,64,128]{2,1,0:T(8,128)(2,1)} custom-call(bf16[8,64,128]{2,1,0:T(8,128)(2,1)} %cand_in.1, bf16[8,64,1024]{2,1,0:T(8,128)(2,1)} %behaviors_in.1, s32[8]{0:T(128)} %lengths.1, bf16[64,2048]{1,0:T(8,128)(2,1)} %bilinear_in.1, f32[8,256]{1,0:T(8,128)} %reshape.3.gain, bf16[256,256]{1,0:T(8,128)(2,1)} %w_gate_in.1, ...), custom_call_target="tpu_custom_call" | custom-call | tf_op jit(solution)/shard_map/pallas_call | solution.py:466
  109.5 1.6 %copy.10 = bf16[8,64,128]{2,1,0:T(8,128)(2,1)} copy(bf16[8,64,128]{2,1,0:T(8,128)(2,1)} %shard_map.82) | data formatting | bytes 262144

commit v3 on v2

--- a/solution.py
+++ b/solution.py
@@ -27,8 +27,12 @@
     key=lambda d: (-min(d[0], 4 - d[0]) - min(d[1], 4 - d[1]), d),
 )
 LEAD = 0
-LAST_HOP = 9
-TICK = 2
+SECOND_HOP = 8
+LAST_HOP = 6
+MOVE_AT = 3
+MOVE = 20
+CAND_HALVES = 32
+MEAN_HALVES = None
 FEATS = 64
 UNITS = 256
 N_SEMS = 320
@@ -99,25 +103,41 @@
     return y * 2 + x // 2, lax.rem(x, 2) * 2 + core
 
 
-def all_gather(t, slot):
+def all_gather(t, slot, halves=None):
+    def block(da, db):
+        return slot(lax.rem(t.a + da + 4, 4), lax.rem(t.b + db + 4, 4))
+
     def whole(da, db, dev):
-        ref = slot(lax.rem(t.a + da + 4, 4), lax.rem(t.b + db + 4, 4))
+        ref = block(da, db)
         return t.send(ref, ref, dev)
 
+    def part(da, db, h, dev):
+        ref = block(da, db).at[pl.ds(h * halves, halves), :]
+        return t.send(ref, ref, dev)
+
     twin = t.partner()
+    far = (2, 1, -1) if halves is None else (1, -1)
     row = {d: whole(0, 0, t.dev_a(d)) for d in (2, 1, -1)}
-    column = {(0, d): whole(0, 0, t.dev_b(d)) for d in (2, 1, -1)}
+    column = {(0, d): whole(0, 0, t.dev_b(d)) for d in far}
     twins = [whole(0, 0, twin)]
     for q in (-1, 1, 2):
         yield
         row[q].wait_recv()
-        for d in (2, 1, -1):
+        for d in far:
             column[-q, d] = whole(-q, 0, t.dev_b(d))
         twins.append(whole(-q, 0, twin))
+    ends = {}
     for (q, d), copy in column.items():
         yield
         copy.wait_recv()
+        if halves is not None:
+            ends.setdefault(q, []).append(part(q, -d, 0 if d == 1 else 1, t.dev_b(d)))
         twins.append(whole(q, -d, twin))
+    for q, copies in ends.items():
+        yield
+        for copy in copies:
+            copy.wait_recv()
+        twins.append(whole(q, 2, twin))
     yield
     for copy in twins:
         copy.wait_recv()
@@ -203,7 +223,7 @@
             tick()
 
 
-def attend(t, mem, w):
+def attend(t, mem, w, beside):
     u = t.user
     copies = []
     for dy, dx, dc in OTHERS:
@@ -212,6 +232,7 @@
             copies.append((dy, dx, t.send(mem.query.at[owned(y, x, c)[0]], mem.keys.at[t.me], (t.z, y, x, c))))
     mem.keys[t.me] = mem.query[u]
     twins = [t.send(mem.keys.at[t.me], mem.keys.at[t.me], t.partner())]
+    beside()
     w.hop()
     for dy, dx, copy in reversed(copies):
         copy.wait_recv()
@@ -285,7 +306,7 @@
         user, quarter = owned(*t.chip(a, b), t.c)
         return mem.pooled.at[h, quarter, user]
 
-    yield from all_gather(t, pooled_slot)
+    yield from all_gather(t, pooled_slot, MEAN_HALVES)
     if h == 0:
         w.wait()
 
@@ -397,7 +418,7 @@
     to_move = list(OTHERS)
     mem.moved = []
 
-    def move_behaviors(count=TICK):
+    def move_behaviors(count):
         for _ in range(min(count, len(to_move))):
             y, x, c = t.shifted(*to_move.pop(0))
             mem.moved.append(t.send(behaviors_of(y, x, c), behaviors.at[t.me], (t.z, y, x, c)))
@@ -412,12 +433,12 @@
     w = Weights(t, weights)
     for copy in cand_copies:
         copy.wait()
-    gathers = [all_gather(t, cand_slot(h)) for h in range(CHUNKS)]
+    gathers = [all_gather(t, cand_slot(h), CAND_HALVES) for h in range(CHUNKS)]
     for one in gathers:
         next(one)
-    move_behaviors()
-
-    own_gain = jnp.broadcast_to(gain[pl.ds(t.z, 1), :], (128, UNITS)).T
+
+    own_gain = gain[pl.ds(pl.multiple_of(t.z * UNITS, UNITS), UNITS)].reshape(1, UNITS)
+    own_gain = jnp.broadcast_to(own_gain, (128, UNITS)).T
     own_gain = jnp.concatenate([own_gain, own_gain], axis=1)
     for i in range(3):
         weight_copies[i].wait()
@@ -426,15 +447,22 @@
         weights[t.z, :, pl.ds(i * UNITS, UNITS)] = v.astype(BF)
     w.hop()
 
-    together(gathers, move_behaviors)
-    move_behaviors(len(to_move))
+    steps = iter(range(1, 99))
+
+    def beside():
+        step = next(steps)
+        if step == MOVE_AT:
+            move_behaviors(MOVE)
+        if step == SECOND_HOP:
+            w.hop()
+
+    together(gathers, beside)
     bilinear_copy.wait()
     for h in range(CHUNKS):
         q = dot(bilinear[...], cands[h].reshape(WIDTH, TOKENS)).astype(BF)
         for u in range(CHUNK_USERS):
             query[h * CHUNK_USERS + u] = q[:, u * CANDS : (u + 1) * CANDS]
-    attend(t, mem, w)
-    w.hop()
+    attend(t, mem, w, lambda: move_behaviors(len(to_move)))
     together([chain(t, h, mem, w) for h in range(CHUNKS)], w.late_hop, LEAD)
     for u in range(USERS_HERE):
         parts = [result[h, :, pl.ds(u // 2 * 128, 128)] for h in range(CHUNKS)]
@@ -499,7 +527,7 @@
         behaviors,
         lengths,
         bilinear,
-        norm_gain.reshape(8, 256),
+        norm_gain,
         w_gate,
         w_up,
         w_down,

time: 112 us -> 105 us (0.938)
  Pallas kernels: 108 us -> 103 us
  local copies, waits for them, and re-layouts: 2.87 us -> 1.57 us
    pallas_call x1, Pallas kernels: 108 us -> 103 us  [shards(): pl.pallas_call(kernel, out_shape=jax.ShapeDtypeStruct(candidates.shape, B...]
    reshape x1 -> x0, local copies, waits for them, and re-layouts: 1.3 us -> none  [shards(): norm_gain.reshape(8, 256)]
where the time goes in v3:
time: 105 us
  Pallas kernels  103 us (98%)
  local copies, waits for them, and re-layouts  1.57 us (1%)
    pallas_call x1, Pallas kernels, shards(): pl.pallas_call(kernel, out_shape=jax.ShapeDtypeStruct(candidates.shape, B...  103 us

profile of v3, /device:TPU:8, one launch (start us, length us, event | category | flops | bytes accessed | tf_op | source)
XLA Modules:
  0.0 104.8 jit_solution(5715933453062289716)
XLA Ops:
  0.0 103.3 %shard_map.82 = bf16[8,64,128]{2,1,0:T(8,128)(2,1)} custom-call(bf16[8,64,128]{2,1,0:T(8,128)(2,1)} %cand_in.1, bf16[8,64,1024]{2,1,0:T(8,128)(2,1)} %behaviors_in.1, s32[8]{0:T(128)} %lengths.1, bf16[64,2048]{1,0:T(8,128)(2,1)} %bilinear_in.1, f32[2048]{0:T(1024)} %gain.1, bf16[256,256]{1,0:T(8,128)(2,1)} %w_gate_in.1, bf16[256,256]{1,0:T(8,128)(2,1)} %w_up_in.1, ...), custom_call_target="tpu_custom_call" | custom-call | tf_op jit(solution)/shard_map/pallas_call | solution.py:494
  103.3 1.6 %copy.10 = bf16[8,64,128]{2,1,0:T(8,128)(2,1)} copy(bf16[8,64,128]{2,1,0:T(8,128)(2,1)} %shard_map.82) | data formatting | bytes 262144

commit v4 on v3

--- a/solution.py
+++ b/solution.py
@@ -29,13 +29,12 @@
 LEAD = 0
 SECOND_HOP = 8
 LAST_HOP = 6
-MOVE_AT = 3
-MOVE = 20
+MOVES = (0, 0, 0, 20)
 CAND_HALVES = 32
 MEAN_HALVES = None
 FEATS = 64
 UNITS = 256
-N_SEMS = 320
+N_OUT, N_INTO = 43, 126
 
 
 class Torus:
@@ -49,7 +48,8 @@
         self.me = (self.y * 4 + self.x) * 2 + self.c
         self.user, self.quarter = owned(self.y, self.x, self.c)
         self.send_sem, self.recv_sem = send_sem, recv_sem
-        self.copies = []
+        self.copies, self.ends = [], []
+        self.outs = self.intos = 0
 
     def chip(self, a, b):
         return b + self.c * (a - b), a + self.c * (b - a)
@@ -72,22 +72,41 @@
     def partner(self):
         return (self.z, self.y, self.x, 1 - self.c)
 
-    def send(self, src, dst, dev):
-        i = len(self.copies)
-        copy = pltpu.make_async_remote_copy(
+    def new_out(self):
+        self.outs += 1
+        return self.outs - 1
+
+    def new_into(self):
+        self.intos += 1
+        return self.intos - 1
+
+    def copy(self, src, dst, dev, out, into):
+        return pltpu.make_async_remote_copy(
             src_ref=src,
             dst_ref=dst,
-            send_sem=self.send_sem.at[i],
-            recv_sem=self.recv_sem.at[i],
+            send_sem=self.send_sem.at[out],
+            recv_sem=self.recv_sem.at[into],
             device_id=dev,
             device_id_type=MESH,
         )
+
+    def send(self, src, dst, dev, out=None, into=None):
+        alone = out is None
+        out = self.new_out() if alone else out
+        copy = self.copy(src, dst, dev, out, self.new_into() if into is None else into)
         copy.start()
-        self.copies.append(copy)
+        if alone:
+            self.copies.append(copy)
         return copy
 
+    def await_all(self, ref, into):
+        self.copy(ref, ref, self.partner(), 0, into).wait_recv()
+
+    def await_sent(self, ref, out):
+        self.ends.append(self.copy(ref, ref, self.partner(), out, 0))
+
     def finish(self):
-        for copy in self.copies:
+        for copy in self.copies + self.ends:
             copy.wait_send()
 
     def barrier(self):
@@ -103,44 +122,49 @@
     return y * 2 + x // 2, lax.rem(x, 2) * 2 + core
 
 
-def all_gather(t, slot, halves=None):
+def all_gather(t, slot, blocks, halves=None):
+    out, into = t.new_out(), t.new_into()
+
     def block(da, db):
         return slot(lax.rem(t.a + da + 4, 4), lax.rem(t.b + db + 4, 4))
 
     def whole(da, db, dev):
         ref = block(da, db)
-        return t.send(ref, ref, dev)
+        return t.send(ref, ref, dev, out)
+
+    def double(da, db):
+        ref = block(da, db)
+        t.send(ref, ref, t.partner(), out, into)
 
     def part(da, db, h, dev):
         ref = block(da, db).at[pl.ds(h * halves, halves), :]
-        return t.send(ref, ref, dev)
-
-    twin = t.partner()
+        return t.send(ref, ref, dev, out)
+
     far = (2, 1, -1) if halves is None else (1, -1)
     row = {d: whole(0, 0, t.dev_a(d)) for d in (2, 1, -1)}
     column = {(0, d): whole(0, 0, t.dev_b(d)) for d in far}
-    twins = [whole(0, 0, twin)]
+    double(0, 0)
     for q in (-1, 1, 2):
         yield
         row[q].wait_recv()
         for d in far:
             column[-q, d] = whole(-q, 0, t.dev_b(d))
-        twins.append(whole(-q, 0, twin))
+        double(-q, 0)
     ends = {}
     for (q, d), copy in column.items():
         yield
         copy.wait_recv()
         if halves is not None:
             ends.setdefault(q, []).append(part(q, -d, 0 if d == 1 else 1, t.dev_b(d)))
-        twins.append(whole(q, -d, twin))
+        double(q, -d)
     for q, copies in ends.items():
         yield
         for copy in copies:
             copy.wait_recv()
-        twins.append(whole(q, 2, twin))
+        double(q, 2)
     yield
-    for copy in twins:
-        copy.wait_recv()
+    t.await_all(blocks(16), into)
+    t.await_sent(blocks(31), out)
 
 
 def ring_sum(t, p, dev, terms, tx, rx):
@@ -226,24 +250,28 @@
 def attend(t, mem, w, beside):
     u = t.user
     copies = []
+    out, into = t.new_out(), t.new_into()
+
+    def double(ref):
+        t.send(ref, ref, t.partner(), out, into)
+
     for dy, dx, dc in OTHERS:
         if dc == 0:
             y, x, c = t.shifted(dy, dx, dc)
-            copies.append((dy, dx, t.send(mem.query.at[owned(y, x, c)[0]], mem.keys.at[t.me], (t.z, y, x, c))))
+            copies.append((dy, dx, t.send(mem.query.at[owned(y, x, c)[0]], mem.keys.at[t.me], (t.z, y, x, c), out)))
     mem.keys[t.me] = mem.query[u]
-    twins = [t.send(mem.keys.at[t.me], mem.keys.at[t.me], t.partner())]
+    double(mem.keys.at[t.me])
     beside()
     w.hop()
     for dy, dx, copy in reversed(copies):
         copy.wait_recv()
         y, x = lax.rem(t.y - dy + 4, 4), lax.rem(t.x - dx + 4, 4)
-        ref = mem.keys.at[(y * 4 + x) * 2 + t.c]
-        twins.append(t.send(ref, ref, t.partner()))
-    for copy in mem.moved:
-        copy.wait_recv()
+        double(mem.keys.at[(y * 4 + x) * 2 + t.c])
+    t.await_all(mem.behaviors.at[pl.ds(0, 31)], mem.move_into)
+    t.await_sent(mem.behaviors.at[pl.ds(0, 31)], mem.move_out)
     mem.own_behaviors.wait()
-    for copy in twins:
-        copy.wait_recv()
+    t.await_all(mem.keys.at[pl.ds(0, 16)], into)
+    t.await_sent(mem.keys.at[pl.ds(0, 31)], out)
     behaviors = mem.behaviors[...].reshape(WIDTH, QUARTER)
     s = dot(mem.keys[...].reshape(WIDTH, CANDS), behaviors, ((0,), (0,)))
     s = s * (1.0 / math.sqrt(WIDTH))
@@ -300,13 +328,15 @@
     for i in (2, 1, 0):
         copies[i].wait_recv()
         total += mem.mean_rx[h, i].astype(F32) * share(i + 1)
-    mem.pooled[h, t.quarter, t.user] = total.astype(BF)
+    mem.pooled[h, t.quarter * USERS_HERE + t.user] = total.astype(BF)
 
     def pooled_slot(a, b):
         user, quarter = owned(*t.chip(a, b), t.c)
-        return mem.pooled.at[h, quarter, user]
-
-    yield from all_gather(t, pooled_slot, MEAN_HALVES)
+        return mem.pooled.at[h, quarter * USERS_HERE + user]
+
+    yield from all_gather(
+        t, pooled_slot, lambda n: mem.pooled.at[h, pl.ds(0, n)], MEAN_HALVES
+    )
     if h == 0:
         w.wait()
 
@@ -315,7 +345,7 @@
         acc = jnp.zeros((n, 2 * UNITS), F32)
         squares = jnp.zeros((n, 1), F32)
         for k in range(4):
-            x = mem.pooled[h, k, pl.ds(4 * i, 4)].reshape(n, FEATURES)
+            x = mem.pooled[h, pl.ds(USERS_HERE * k + 4 * i, 4)].reshape(n, FEATURES)
             acc += dot(x, mem.weights[pl.ds(2 * k, 2), :, pl.ds(0, 2 * UNITS)].reshape(FEATURES, 2 * UNITS))
             v = x.astype(F32)
             squares += jnp.sum(v * v, axis=1, keepdims=True)
@@ -416,12 +446,13 @@
     t.barrier()
 
     to_move = list(OTHERS)
-    mem.moved = []
+    mem.move_out, mem.move_into = t.new_out(), t.new_into()
 
     def move_behaviors(count):
         for _ in range(min(count, len(to_move))):
             y, x, c = t.shifted(*to_move.pop(0))
-            mem.moved.append(t.send(behaviors_of(y, x, c), behaviors.at[t.me], (t.z, y, x, c)))
+            src, dst = behaviors_of(y, x, c), behaviors.at[t.me]
+            t.send(src, dst, (t.z, y, x, c), mem.move_out, mem.move_into)
 
     def cand_slot(h):
         def slot(a, b):
@@ -433,7 +464,10 @@
     w = Weights(t, weights)
     for copy in cand_copies:
         copy.wait()
-    gathers = [all_gather(t, cand_slot(h), CAND_HALVES) for h in range(CHUNKS)]
+    gathers = [
+        all_gather(t, cand_slot(h), lambda n, h=h: cands.at[h, pl.ds(0, n)], CAND_HALVES)
+        for h in range(CHUNKS)
+    ]
     for one in gathers:
         next(one)
 
@@ -451,11 +485,12 @@
 
     def beside():
         step = next(steps)
-        if step == MOVE_AT:
-            move_behaviors(MOVE)
+        if step < len(MOVES):
+            move_behaviors(MOVES[step])
         if step == SECOND_HOP:
             w.hop()
 
+    move_behaviors(MOVES[0])
     together(gathers, beside)
     bilinear_copy.wait()
     for h in range(CHUNKS):
@@ -472,6 +507,7 @@
             both = jnp.concatenate([part[:, ROWS:] for part in parts], axis=1)
         out[u] = both.astype(BF)
     t.finish()
+    assert (t.outs, t.intos) == (N_OUT, N_INTO), (t.outs, t.intos)
 
 
 def exchange_buffers(rows, piece, width):
@@ -511,12 +547,12 @@
             pltpu.VMEM((8, CANDS), F32),
             pltpu.VMEM((3, 8, CANDS), F32),
             pltpu.VMEM((4, CANDS, 128), F32),
-            pltpu.VMEM((CHUNKS, 4, USERS_HERE, ROWS, FEATURES), BF),
+            pltpu.VMEM((CHUNKS, 4 * USERS_HERE, ROWS, FEATURES), BF),
             pltpu.VMEM((CHUNKS, UNITS, TOKENS), BF),
             pltpu.VMEM((CHUNKS, FEATS, TOKENS), F32),
             *exchange_buffers(256, FEATS, TOKENS),
-            pltpu.SemaphoreType.DMA((N_SEMS,)),
-            pltpu.SemaphoreType.DMA((N_SEMS,)),
+            pltpu.SemaphoreType.DMA((N_OUT,)),
+            pltpu.SemaphoreType.DMA((N_INTO,)),
             pltpu.SemaphoreType.DMA((16,)),
         ],
         compiler_params=pltpu.CompilerParams(

time: 105 us -> 100 us (0.952)
  Pallas kernels: 103 us -> 98.6 us
    pallas_call x1, Pallas kernels: 103 us -> 98.6 us  [shards(): pl.pallas_call(kernel, out_shape=jax.ShapeDtypeStruct(candidates.shape, B...]
where the time goes in v4:
time: 100 us
  Pallas kernels  98.6 us (99%)
  local copies, waits for them, and re-layouts  1.57 us (2%)
    pallas_call x1, Pallas kernels, shards(): pl.pallas_call(kernel, out_shape=jax.ShapeDtypeStruct(candidates.shape, B...  98.6 us

profile of v4, /device:TPU:8, one launch (start us, length us, event | category | flops | bytes accessed | tf_op | source)
XLA Modules:
  0.0 100.2 jit_solution(13037264116423863489)
XLA Ops:
  0.0 98.6 %shard_map.82 = bf16[8,64,128]{2,1,0:T(8,128)(2,1)} custom-call(bf16[8,64,128]{2,1,0:T(8,128)(2,1)} %cand_in.1, bf16[8,64,1024]{2,1,0:T(8,128)(2,1)} %behaviors_in.1, s32[8]{0:T(128)} %lengths.1, bf16[64,2048]{1,0:T(8,128)(2,1)} %bilinear_in.1, f32[2048]{0:T(1024)} %gain.1, bf16[256,256]{1,0:T(8,128)(2,1)} %w_gate_in.1, bf16[256,256]{1,0:T(8,128)(2,1)} %w_up_in.1, ...), custom_call_target="tpu_custom_call" | custom-call | tf_op jit(solution)/shard_map/pallas_call | solution.py:530
  98.7 1.6 %copy.10 = bf16[8,64,128]{2,1,0:T(8,128)(2,1)} copy(bf16[8,64,128]{2,1,0:T(8,128)(2,1)} %shard_map.82) | data formatting | bytes 262144

commit v5 on v4

--- a/solution.py
+++ b/solution.py
@@ -28,13 +28,13 @@
 )
 LEAD = 0
 SECOND_HOP = 8
-LAST_HOP = 6
-MOVES = (0, 0, 0, 20)
+LAST_HOP = 4
+MOVES = (4, 0, 0, 5, 5, 5, 5, 5, 5)
 CAND_HALVES = 32
-MEAN_HALVES = None
+MEAN_HALVES = 32
 FEATS = 64
 UNITS = 256
-N_OUT, N_INTO = 43, 126
+N_OUT, N_INTO = 43, 134
 
 
 class Torus:
@@ -141,7 +141,7 @@
         return t.send(ref, ref, dev, out)
 
     far = (2, 1, -1) if halves is None else (1, -1)
-    row = {d: whole(0, 0, t.dev_a(d)) for d in (2, 1, -1)}
+    row = {d: whole(0, 0, t.dev_a(d)) for d in (1, -1, 2)}
     column = {(0, d): whole(0, 0, t.dev_b(d)) for d in far}
     double(0, 0)
     for q in (-1, 1, 2):

time: 100 us -> 96.6 us (0.966); the launches traced: 100 us -> 95.4 us
  Pallas kernels: 98.6 us -> 93.8 us
    pallas_call x1, Pallas kernels: 98.6 us -> 93.8 us  [shards(): pl.pallas_call(kernel, out_shape=jax.ShapeDtypeStruct(candidates.shape, B...]
where the time goes in v5:
time: 96.6 us; the launch traced here: 95.4 us
  Pallas kernels  93.8 us (97%)
  local copies, waits for them, and re-layouts  1.57 us (2%)
    pallas_call x1, Pallas kernels, shards(): pl.pallas_call(kernel, out_shape=jax.ShapeDtypeStruct(candidates.shape, B...  93.8 us

profile of v5, /device:TPU:8, one launch (start us, length us, event | category | flops | bytes accessed | tf_op | source)
XLA Modules:
  0.0 95.4 jit_solution(14503013548942788674)
XLA Ops:
  0.0 93.8 %shard_map.82 = bf16[8,64,128]{2,1,0:T(8,128)(2,1)} custom-call(bf16[8,64,128]{2,1,0:T(8,128)(2,1)} %cand_in.1, bf16[8,64,1024]{2,1,0:T(8,128)(2,1)} %behaviors_in.1, s32[8]{0:T(128)} %lengths.1, bf16[64,2048]{1,0:T(8,128)(2,1)} %bilinear_in.1, f32[2048]{0:T(1024)} %gain.1, bf16[256,256]{1,0:T(8,128)(2,1)} %w_gate_in.1, bf16[256,256]{1,0:T(8,128)(2,1)} %w_up_in.1, ...), custom_call_target="tpu_custom_call" | custom-call | tf_op jit(solution)/shard_map/pallas_call | solution.py:530
  93.8 1.6 %copy.10 = bf16[8,64,128]{2,1,0:T(8,128)(2,1)} copy(bf16[8,64,128]{2,1,0:T(8,128)(2,1)} %shard_map.82) | data formatting | bytes 262144

commit v6 on v5

--- a/solution.py
+++ b/solution.py
@@ -29,7 +29,7 @@
 LEAD = 0
 SECOND_HOP = 8
 LAST_HOP = 4
-MOVES = (4, 0, 0, 5, 5, 5, 5, 5, 5)
+MOVES = (6, 0, 4, 7, 7, 7)
 CAND_HALVES = 32
 MEAN_HALVES = 32
 FEATS = 64
@@ -115,7 +115,7 @@
         peers += [(self.z, *self.shifted(*d)) for d in OTHERS]
         for dev in peers:
             pl.semaphore_signal(sem, inc=1, device_id=dev, device_id_type=MESH)
-        pl.semaphore_wait(sem, len(peers))
+        return lambda: pl.semaphore_wait(sem, len(peers))
 
 
 def owned(y, x, core):
@@ -409,6 +409,7 @@
 ):
     send_sem, recv_sem, in_sem = rest[-3:]
     t = Torus(send_sem, recv_sem)
+    entered = t.barrier()
     mem = Memory()
     mem.behaviors, mem.bilinear, mem.weights, mem.cands = behaviors, bilinear, weights, cands
     mem.query, mem.keys, mem.pooled, mem.hidden = query, keys, pooled, hidden
@@ -443,7 +444,7 @@
         return behaviors_in.at[user, :, pl.ds(at, QUARTER)]
 
     mem.own_behaviors = fetch(behaviors_of(t.y, t.x, t.c), behaviors.at[t.me])
-    t.barrier()
+    entered()
 
     to_move = list(OTHERS)
     mem.move_out, mem.move_into = t.new_out(), t.new_into()

time: 96.6 us -> 96.2 us (level)
  no operation moved by 1% of the time
where the time goes in v6:
time: 96.2 us; the launch traced here: 95 us
  Pallas kernels  93.4 us (97%)
  local copies, waits for them, and re-layouts  1.57 us (2%)
    pallas_call x1, Pallas kernels, shards(): pl.pallas_call(kernel, out_shape=jax.ShapeDtypeStruct(candidates.shape, B...  93.4 us

profile of v6, /device:TPU:8, one launch (start us, length us, event | category | flops | bytes accessed | tf_op | source)
XLA Modules:
  0.0 95.0 jit_solution(12114890853428339079)
XLA Ops:
  0.0 93.4 %shard_map.82 = bf16[8,64,128]{2,1,0:T(8,128)(2,1)} custom-call(bf16[8,64,128]{2,1,0:T(8,128)(2,1)} %cand_in.1, bf16[8,64,1024]{2,1,0:T(8,128)(2,1)} %behaviors_in.1, s32[8]{0:T(128)} %lengths.1, bf16[64,2048]{1,0:T(8,128)(2,1)} %bilinear_in.1, f32[2048]{0:T(1024)} %gain.1, bf16[256,256]{1,0:T(8,128)(2,1)} %w_gate_in.1, bf16[256,256]{1,0:T(8,128)(2,1)} %w_up_in.1, ...), custom_call_target="tpu_custom_call" | custom-call | tf_op jit(solution)/shard_map/pallas_call | solution.py:531
  93.4 1.6 %copy.10 = bf16[8,64,128]{2,1,0:T(8,128)(2,1)} copy(bf16[8,64,128]{2,1,0:T(8,128)(2,1)} %shard_map.82) | data formatting | bytes 262144
